TPU v7x, 32 devices: a whole 2x2x4 slice. The times are simulated.
32 devices in a mesh: gx: 4 (over y, x), gy: 4 (over z), gz: 2 (over core).
Axes of the slice: x: 2, y: 2, z: 4, core: 2. Of those that a mesh axis runs over, the one named last changes fastest.
Arguments:
- right_side: float32 [64, 256, 1024], P('gx', 'gy', 'gz'), may hold values from -24 to 24
- reaction: float32 [64, 256, 1024], P('gx', 'gy', 'gz'), may hold values from 0.5 to 2
- velocity: float32 [3, 64, 256, 1024], P(None, 'gx', 'gy', 'gz'), may hold values from -0.5 to 0.5
Outputs:
- solution: float32 [64, 256, 1024], P('gx', 'gy', 'gz')
- residual: float32 [64, 256, 1024], P('gx', 'gy', 'gz')
- residual_norm: float32 [], replicated
All inputs are finite; a program needn't handle non-finite values.
Results may differ from a plain program's by a relative error of at most 0.00002.
Values sent between devices are 32-bit elements; how exact they have to be, the bound alone decides.
A program may use at most 128 MiB of HBM per device.

v0:
```python
import functools
import itertools

import jax
import jax.numpy as jnp
from jax import lax
from jax.experimental import pallas as pl
from jax.experimental.pallas import tpu as pltpu
from jax.sharding import PartitionSpec as P

ITERS = 5
CHUNKS = 4
ROWS = 8

centre = 7.25
half_width = 6.75

AXES = ("gx", "gy", "gz")
PY, PZ = 8, 128
LOW, HIGH, INNER = 0, 1, 2


def chebyshev_weights(count):
    ratio_value = centre / half_width
    weights = [1.0 / ratio_value]
    for iteration in range(count):
        weights.append(1.0 / (2.0 * ratio_value - weights[-1]))
    return weights


PHASES = ((2,), (0, 1))


def phase_steps(sizes, axes):
    ranges = [range(n) if i in axes else (0,) for i, n in enumerate(sizes)]
    return [steps for steps in itertools.product(*ranges) if any(steps)]


def greeted_by(sizes):
    steps = {
        tuple(p if j == i else 0 for j in range(len(sizes)))
        for i, n in enumerate(sizes)
        for p in (1, n - 1)
    }
    if sizes[0] // 2 + sizes[1] - 1 + sizes[2] - 1 <= ITERS + 1:
        return sorted(steps)
    for axes in PHASES:
        steps |= set(phase_steps(sizes, axes))
    return sorted(steps)


def phase_slots(sizes):
    return sum(len(phase_steps(sizes, axes)) + 1 for axes in PHASES)


def kernel(
    sizes,
    rhs,
    reaction,
    velocity,
    sol,
    res,
    norm,
    d,
    reac,
    vel,
    ysend,
    yrecv,
    part,
    load_sem,
    xs_sem,
    xr_sem,
    ys_sem,
    yr_sem,
    zs_sem,
    zr_sem,
    ps_sem,
    pr_sem,
):
    nx, ny, nz = rhs.shape
    weights = chebyshev_weights(ITERS)
    me = [lax.axis_index(a) for a in AXES]
    mid_y = pl.ds(PY, ny)
    mid_z = pl.ds(PZ, nz)
    chunk = ny // CHUNKS

    load_rhs = pltpu.make_async_copy(
        rhs, d.at[0, pl.ds(1, nx), mid_y, mid_z], load_sem.at[0]
    )
    load_rhs.start()
    loads = [pltpu.make_async_copy(reaction, reac, load_sem.at[1])] + [
        pltpu.make_async_copy(velocity.at[i], vel.at[i], load_sem.at[2 + i])
        for i in range(3)
    ]
    for copy in loads:
        copy.start()

    barrier = pltpu.get_barrier_semaphore()
    def shifted(steps):
        return {
            a: lax.rem(i + p, n)
            for a, n, i, p in zip(AXES, sizes, me, steps)
            if p
        }

    greeted = greeted_by(sizes)
    for steps in greeted:
        pl.semaphore_signal(
            barrier,
            inc=1,
            device_id=shifted(steps),
            device_id_type=pl.DeviceIdType.MESH,
        )

    for side, at_edge in ((LOW, me[1] == 0), (HIGH, me[1] == sizes[1] - 1)):
        @pl.when(at_edge)
        def _(side=side):
            for slot in range(2):
                yrecv[slot, side] = jnp.zeros((nx, 1, nz), jnp.float32)

    for first, at_edge in ((0, me[2] == 0), (PZ + nz, me[2] == sizes[2] - 1)):
        @pl.when(at_edge)
        def _(first=first):
            def clear(x, carry):
                for slot in range(2):
                    d[slot, x, pl.ds(PY, ny), pl.ds(first, PZ)] = jnp.zeros(
                        (ny, PZ), jnp.float32
                    )
                return carry

            lax.fori_loop(1, nx + 1, clear, 0)

    pl.semaphore_wait(barrier, len(greeted))

    def remote(src, dst, send, recv, axis, target):
        return pltpu.make_async_remote_copy(
            src_ref=src,
            dst_ref=dst,
            send_sem=send,
            recv_sem=recv,
            device_id={AXES[axis]: target},
            device_id_type=pl.DeviceIdType.MESH,
        )

    def x_copy(slot, side, c, source=None):
        n = sizes[0]
        rows = pl.ds(PY + c * chunk, chunk)
        plane, land, target = (
            (nx, 0, lax.rem(me[0] + 1, n))
            if side == LOW
            else (1, nx + 1, lax.rem(me[0] + n - 1, n))
        )
        if source is None:
            src = d.at[slot, plane, rows, mid_z]
        else:
            src = source.at[plane - 1, pl.ds(c * chunk, chunk), :]
        return remote(
            src,
            d.at[slot, land, rows, mid_z],
            xs_sem.at[slot, side, c],
            xr_sem.at[slot, side, c],
            0,
            target,
        )

    def span(group):
        return {LOW: (0, 1), HIGH: (nx - 1, 1), INNER: (1, nx - 2)}[group]

    def target_of(axis, side):
        n = sizes[axis]
        step = 1 if side == LOW else n - 1
        return lax.rem(me[axis] + step, n)

    def sends(axis, side):
        return me[axis] < sizes[axis] - 1 if side == LOW else me[axis] > 0

    def receives(axis, side):
        return me[axis] > 0 if side == LOW else me[axis] < sizes[axis] - 1

    def y_copy(slot, side, group):
        x = pl.ds(*span(group))
        return remote(
            ysend.at[slot, side, x],
            yrecv.at[slot, side, x],
            ys_sem.at[slot, side, group],
            yr_sem.at[slot, side, group],
            1,
            target_of(1, side),
        )

    def z_copy(slot, side, group):
        first, count = span(group)
        x = pl.ds(first + 1, count)
        source, land = (nz, 0) if side == LOW else (PZ, PZ + nz)
        return remote(
            d.at[slot, x, mid_y, pl.ds(source, PZ)],
            d.at[slot, x, mid_y, pl.ds(land, PZ)],
            zs_sem.at[slot, side, group],
            zr_sem.at[slot, side, group],
            2,
            target_of(2, side),
        )

    def open_each(slot, groups, act):
        for group in groups:
            for axis, copy in ((2, z_copy), (1, y_copy)):
                for side in (LOW, HIGH):
                    rule = receives if act == "wait_recv" else sends

                    @pl.when(rule(axis, side))
                    def _(copy=copy, side=side, group=group):
                        getattr(copy(slot, side, group), act)()

    def pack(slot, x):
        ysend[slot, LOW, x - 1] = d[slot, x, pl.ds(PY + ny - 1, 1), mid_z]
        ysend[slot, HIGH, x - 1] = d[slot, x, pl.ds(PY, 1), mid_z]

    def unpack(slot, x):
        d[slot, x, pl.ds(PY - 1, 1), mid_z] = yrecv[slot, LOW, x - 1]
        d[slot, x, pl.ds(PY + ny, 1), mid_z] = yrecv[slot, HIGH, x - 1]

    def block(k, x, y):
        slot, other = k % 2, (k + 1) % 2
        here = (x - 1, pl.ds(y, ROWS), slice(None))
        rows = pl.ds(PY + y, ROWS)
        mid = d[slot, x, rows, mid_z]
        px = d[slot, x + 1, rows, mid_z]
        mx = d[slot, x - 1, rows, mid_z]
        py = d[slot, x, pl.ds(PY + y + 1, ROWS), mid_z]
        my = d[slot, x, pl.ds(PY + y - 1, ROWS), mid_z]
        wide = nz + PZ
        pz = pltpu.roll(d[slot, x, rows, pl.ds(PZ, wide)], wide - 1, 1)[:, :nz]
        mz = pltpu.roll(d[slot, x, rows, pl.ds(0, wide)], 1, 1)[:, PZ:]
        beside = ((px + mx) + (py + my)) + (pz + mz)
        skew = vel[0, *here] * (px - mx) + vel[1, *here] * (py - my)
        skew = skew + vel[2, *here] * (pz - mz)
        applied = (6.0 + reac[here]) * mid - (beside - skew)
        if k == 0:
            left = mid - (1.0 / centre) * applied
            sol[here] = (1.0 / centre) * mid
        else:
            left = res[here] - applied
            sol[here] = sol[here] + mid
        res[here] = left
        if k + 1 < ITERS:
            keep = weights[k + 1] * weights[k] * (1.0 / centre if k == 0 else 1.0)
            d[other, x, rows, mid_z] = keep * mid + (
                2.0 * weights[k + 1] / half_width
            ) * left
            return None
        return left * left

    def add(total, term):
        return total if term is None else total + term

    for side in (LOW, HIGH):
        for c in range(CHUNKS):
            x_copy(0, side, c, rhs).start()
    load_rhs.wait()

    def pack_first(x, carry):
        pack(0, x)
        return carry

    lax.fori_loop(1, nx + 1, pack_first, 0)
    open_each(0, (INNER, LOW, HIGH), "start")
    for copy in loads:
        copy.wait()

    total = jnp.zeros((ROWS, nz), jnp.float32)
    for k in range(ITERS):
        slot, other = k % 2, (k + 1) % 2
        more = k + 1 < ITERS
        open_each(slot, (INNER,), "wait_recv")
        if k > 0:
            open_each(other, (INNER,), "wait_send")

        def inner(x, total, k=k, slot=slot, other=other, more=more):
            unpack(slot, x)
            for y in range(0, ny, ROWS):
                total = add(total, block(k, x, y))
            if more:
                pack(other, x)
            return total

        total = lax.fori_loop(2, nx, inner, total)
        if more:
            open_each(other, (INNER,), "start")
        open_each(slot, (LOW, HIGH), "wait_recv")
        if k > 0:
            open_each(other, (LOW, HIGH), "wait_send")
        unpack(slot, 1)
        unpack(slot, nx)
        for c in range(CHUNKS):
            for side in (LOW, HIGH):
                x_copy(slot, side, c).wait_recv()
                if k > 0:
                    x_copy(other, side, c, rhs if k == 1 else None).wait_send()
            for x in (1, nx):
                for y in range(c * chunk, (c + 1) * chunk, ROWS):
                    total = add(total, block(k, x, y))
            if more:
                for side in (LOW, HIGH):
                    x_copy(other, side, c).start()
        if more:
            pack(other, 1)
            pack(other, nx)
            open_each(other, (LOW, HIGH), "start")

    tile = total[:, :PZ]
    for z in range(PZ, nz, PZ):
        tile = tile + total[:, z : z + PZ]
    first = 0
    for axes in PHASES:
        group = phase_steps(sizes, axes)
        own = jnp.int32(0)
        for axis in axes:
            own = own * sizes[axis] + me[axis]
        part[first + own] = tile
        copies = [
            pltpu.make_async_remote_copy(
                src_ref=part.at[first + own],
                dst_ref=part.at[first + own],
                send_sem=ps_sem.at[first + p],
                recv_sem=pr_sem.at[first + p],
                device_id=shifted(steps),
                device_id_type=pl.DeviceIdType.MESH,
            )
            for p, steps in enumerate(group)
        ]
        for copy in copies:
            copy.start()
        for copy in copies:
            copy.wait_recv()
        tile = part[first]
        for p in range(1, len(group) + 1):
            tile = tile + part[first + p]
        for copy in copies:
            copy.wait_send()
        first += len(group) + 1
    last = (ITERS - 1) % 2
    open_each(last, (INNER, LOW, HIGH), "wait_send")
    for c in range(CHUNKS):
        for side in (LOW, HIGH):
            x_copy(last, side, c).wait_send()
    cells = nx * ny * nz * sizes[0] * sizes[1] * sizes[2]
    mean = jnp.sum(tile, keepdims=True) / cells
    norm[...] = jnp.sqrt(mean + 1e-06)


def local(sizes, right_side, reaction, velocity):
    nx, ny, nz = right_side.shape
    hbm = pl.BlockSpec(memory_space=pltpu.HBM)
    vmem = pl.BlockSpec(memory_space=pltpu.VMEM)
    dma = pltpu.SemaphoreType.DMA
    field = jax.ShapeDtypeStruct((nx, ny, nz), jnp.float32)
    sol, res, norm = pl.pallas_call(
        functools.partial(kernel, sizes),
        out_shape=(field, field, jax.ShapeDtypeStruct((1, 1), jnp.float32)),
        in_specs=[hbm] * 3,
        out_specs=(vmem, vmem, vmem),
        scratch_shapes=[
            pltpu.VMEM((2, nx + 2, ny + 2 * PY, nz + 2 * PZ), jnp.float32),
            pltpu.VMEM((nx, ny, nz), jnp.float32),
            pltpu.VMEM((3, nx, ny, nz), jnp.float32),
            pltpu.VMEM((2, 2, nx, 1, nz), jnp.float32),
            pltpu.VMEM((2, 2, nx, 1, nz), jnp.float32),
            pltpu.VMEM((phase_slots(sizes), ROWS, PZ), jnp.float32),
            dma((5,)),
            dma((2, 2, CHUNKS)),
            dma((2, 2, CHUNKS)),
            dma((2, 2, 3)),
            dma((2, 2, 3)),
            dma((2, 2, 3)),
            dma((2, 2, 3)),
            dma((phase_slots(sizes),)),
            dma((phase_slots(sizes),)),
        ],
        compiler_params=pltpu.CompilerParams(
            collective_id=0,
            has_side_effects=True,
            vmem_limit_bytes=40 * 1024 * 1024,
        ),
    )(
        *(
            pltpu.with_memory_space_constraint(a, pltpu.HBM)
            for a in (right_side, reaction, velocity)
        )
    )
    return sol, res, norm[0, 0]


def solution(mesh):
    sizes = tuple(mesh.shape[a] for a in AXES)
    return jax.shard_map(
        functools.partial(local, sizes),
        mesh=mesh,
        in_specs=(P("gx", "gy", "gz"), P("gx", "gy", "gz"), P(None, "gx", "gy", "gz")),
        out_specs=(P("gx", "gy", "gz"), P("gx", "gy", "gz"), P()),
        check_vma=False,
    )
```

profile of v0, /device:TPU:0, one launch (start us, length us, event | category | flops | bytes accessed | tf_op | source)
XLA Modules:
  0.0 48.2 jit_solution(17478560248621485291)
XLA Ops:
  0.6 43.3 %shard_map.58 = (f32[16,64,512]{2,1,0:T(8,128)S(1)}, f32[16,64,512]{2,1,0:T(8,128)S(1)}, f32[1,1]{1,0:T(1,128)}) custom-call(f32[16,64,512]{2,1,0:T(8,128)} %rhs.1, f32[16,64,512]{2,1,0:T(8,128)} %reaction.1, f32[3,16,64,512]{3,2,1,0:T(8,128)} %velocity.1), custom_call_target="tpu_custom_call" | custom-call | tf_op jit(solution)/shard_map/pallas_call | solution.py:357
  43.9 1.3 %copy.9 = f32[16,64,512]{2,1,0:T(8,128)} copy(f32[16,64,512]{2,1,0:T(8,128)S(1)} %get-tuple-element.12) | data formatting | bytes 4194304
  45.2 1.3 %copy.10 = f32[16,64,512]{2,1,0:T(8,128)} copy(f32[16,64,512]{2,1,0:T(8,128)S(1)} %get-tuple-element.13) | data formatting | bytes 4194304
where the time goes:
time: 48.4 us; the launch traced here: 48.2 us
  Pallas kernels  43.3 us (89%)
  local copies, waits for them, and re-layouts  2.64 us (5%)
  between operations  2.33 us (5%)
    pallas_call x1, Pallas kernels, local(): pl.pallas_call(functools.partial(kernel, sizes), out_shape=(field, field,...  43.3 us
    unnamed x2, local copies, waits for them, and re-layouts  2.64 us

commit v1 on v0

--- a/solution.py
+++ b/solution.py
@@ -11,13 +11,14 @@
 ITERS = 5
 CHUNKS = 4
 ROWS = 8
+GROUP = 7
 
 centre = 7.25
 half_width = 6.75
 
 AXES = ("gx", "gy", "gz")
 PY, PZ = 8, 128
-LOW, HIGH, INNER = 0, 1, 2
+LOW, HIGH = 0, 1
 
 
 def chebyshev_weights(count):
@@ -28,7 +29,12 @@
     return weights
 
 
-PHASES = ((2,), (0, 1))
+def reaches(sizes):
+    return sizes[0] // 2 + sizes[1] - 1 + sizes[2] - 1 <= ITERS + 1
+
+
+def phases(sizes):
+    return ((0, 1, 2),) if reaches(sizes) else ((2,), (0, 1))
 
 
 def phase_steps(sizes, axes):
@@ -42,15 +48,13 @@
         for i, n in enumerate(sizes)
         for p in (1, n - 1)
     }
-    if sizes[0] // 2 + sizes[1] - 1 + sizes[2] - 1 <= ITERS + 1:
-        return sorted(steps)
-    for axes in PHASES:
+    for axes in phases(sizes):
         steps |= set(phase_steps(sizes, axes))
     return sorted(steps)
 
 
 def phase_slots(sizes):
-    return sum(len(phase_steps(sizes, axes)) + 1 for axes in PHASES)
+    return sum(len(phase_steps(sizes, axes)) + 1 for axes in phases(sizes))
 
 
 def kernel(
@@ -67,6 +71,7 @@
     ysend,
     yrecv,
     part,
+    rhs_sem,
     load_sem,
     xs_sem,
     xr_sem,
@@ -84,16 +89,31 @@
     mid_z = pl.ds(PZ, nz)
     chunk = ny // CHUNKS
 
-    load_rhs = pltpu.make_async_copy(
-        rhs, d.at[0, pl.ds(1, nx), mid_y, mid_z], load_sem.at[0]
-    )
-    load_rhs.start()
-    loads = [pltpu.make_async_copy(reaction, reac, load_sem.at[1])] + [
-        pltpu.make_async_copy(velocity.at[i], vel.at[i], load_sem.at[2 + i])
-        for i in range(3)
+    order = [0, CHUNKS - 1] + list(range(1, CHUNKS - 1))
+    load_rhs = [
+        pltpu.make_async_copy(
+            rhs.at[pl.ds(first, count)],
+            d.at[0, pl.ds(1 + first, count), mid_y, mid_z],
+            rhs_sem.at[i],
+        )
+        for i, (first, count) in enumerate(((0, 1), (nx - 1, 1), (1, nx - 2)))
     ]
-    for copy in loads:
+    loads = {}
+    for c in order:
+        rows = pl.ds(c * chunk, chunk)
+        loads[c] = [
+            pltpu.make_async_copy(
+                reaction.at[:, rows], reac.at[:, rows], load_sem.at[c, 0]
+            ),
+            pltpu.make_async_copy(
+                velocity.at[:, :, rows], vel.at[:, :, rows], load_sem.at[c, 1]
+            ),
+        ]
+    for copy in load_rhs:
         copy.start()
+    for c in order:
+        for copy in loads[c]:
+            copy.start()
 
     barrier = pltpu.get_barrier_semaphore()
     def shifted(steps):
@@ -103,14 +123,32 @@
             if p
         }
 
-    greeted = greeted_by(sizes)
-    for steps in greeted:
+    def greet(steps):
         pl.semaphore_signal(
             barrier,
             inc=1,
             device_id=shifted(steps),
             device_id_type=pl.DeviceIdType.MESH,
         )
+
+    if reaches(sizes):
+        for step in sorted({1, sizes[0] - 1}):
+            greet((step, 0, 0))
+        greeters = len({1, sizes[0] - 1})
+        for axis in (1, 2):
+            for step, there in (
+                (1, me[axis] < sizes[axis] - 1),
+                (sizes[axis] - 1, me[axis] > 0),
+            ):
+                @pl.when(there)
+                def _(axis=axis, step=step):
+                    greet(tuple(step if a == axis else 0 for a in range(3)))
+
+                greeters = greeters + there.astype(jnp.int32)
+    else:
+        for steps in greeted_by(sizes):
+            greet(steps)
+        greeters = len(greeted_by(sizes))
 
     for side, at_edge in ((LOW, me[1] == 0), (HIGH, me[1] == sizes[1] - 1)):
         @pl.when(at_edge)
@@ -130,7 +168,7 @@
 
             lax.fori_loop(1, nx + 1, clear, 0)
 
-    pl.semaphore_wait(barrier, len(greeted))
+    pl.semaphore_wait(barrier, greeters)
 
     def remote(src, dst, send, recv, axis, target):
         return pltpu.make_async_remote_copy(
@@ -142,7 +180,7 @@
             device_id_type=pl.DeviceIdType.MESH,
         )
 
-    def x_copy(slot, side, c, source=None):
+    def x_copy(slot, side, c):
         n = sizes[0]
         rows = pl.ds(PY + c * chunk, chunk)
         plane, land, target = (
@@ -150,12 +188,8 @@
             if side == LOW
             else (1, nx + 1, lax.rem(me[0] + n - 1, n))
         )
-        if source is None:
-            src = d.at[slot, plane, rows, mid_z]
-        else:
-            src = source.at[plane - 1, pl.ds(c * chunk, chunk), :]
         return remote(
-            src,
+            d.at[slot, plane, rows, mid_z],
             d.at[slot, land, rows, mid_z],
             xs_sem.at[slot, side, c],
             xr_sem.at[slot, side, c],
@@ -163,9 +197,6 @@
             target,
         )
 
-    def span(group):
-        return {LOW: (0, 1), HIGH: (nx - 1, 1), INNER: (1, nx - 2)}[group]
-
     def target_of(axis, side):
         n = sizes[axis]
         step = 1 if side == LOW else n - 1
@@ -177,47 +208,54 @@
     def receives(axis, side):
         return me[axis] > 0 if side == LOW else me[axis] < sizes[axis] - 1
 
-    def y_copy(slot, side, group):
-        x = pl.ds(*span(group))
+    def y_copy(slot, side):
         return remote(
-            ysend.at[slot, side, x],
-            yrecv.at[slot, side, x],
-            ys_sem.at[slot, side, group],
-            yr_sem.at[slot, side, group],
+            ysend.at[slot, side],
+            yrecv.at[slot, side],
+            ys_sem.at[slot, side],
+            yr_sem.at[slot, side],
             1,
             target_of(1, side),
         )
 
-    def z_copy(slot, side, group):
-        first, count = span(group)
-        x = pl.ds(first + 1, count)
+    def z_copy(slot, side, c):
+        x = pl.ds(1, nx)
+        rows = pl.ds(PY + c * chunk, chunk)
         source, land = (nz, 0) if side == LOW else (PZ, PZ + nz)
         return remote(
-            d.at[slot, x, mid_y, pl.ds(source, PZ)],
-            d.at[slot, x, mid_y, pl.ds(land, PZ)],
-            zs_sem.at[slot, side, group],
-            zr_sem.at[slot, side, group],
+            d.at[slot, x, rows, pl.ds(source, PZ)],
+            d.at[slot, x, rows, pl.ds(land, PZ)],
+            zs_sem.at[slot, side, c],
+            zr_sem.at[slot, side, c],
             2,
             target_of(2, side),
         )
 
-    def open_each(slot, groups, act):
-        for group in groups:
-            for axis, copy in ((2, z_copy), (1, y_copy)):
-                for side in (LOW, HIGH):
-                    rule = receives if act == "wait_recv" else sends
-
-                    @pl.when(rule(axis, side))
-                    def _(copy=copy, side=side, group=group):
-                        getattr(copy(slot, side, group), act)()
-
-    def pack(slot, x):
-        ysend[slot, LOW, x - 1] = d[slot, x, pl.ds(PY + ny - 1, 1), mid_z]
-        ysend[slot, HIGH, x - 1] = d[slot, x, pl.ds(PY, 1), mid_z]
-
-    def unpack(slot, x):
-        d[slot, x, pl.ds(PY - 1, 1), mid_z] = yrecv[slot, LOW, x - 1]
-        d[slot, x, pl.ds(PY + ny, 1), mid_z] = yrecv[slot, HIGH, x - 1]
+    def open_each(slot, c, act):
+        rule = receives if act == "wait_recv" else sends
+        for side in (LOW, HIGH):
+            row_in = CHUNKS - 1 if side == LOW and act != "wait_recv" else 0
+
+            @pl.when(rule(2, side))
+            def _(side=side):
+                getattr(z_copy(slot, side, c), act)()
+
+            if c == row_in:
+                @pl.when(rule(1, side))
+                def _(side=side):
+                    getattr(y_copy(slot, side), act)()
+
+    def pack(slot, x, c):
+        if c == CHUNKS - 1:
+            ysend[slot, LOW, x - 1] = d[slot, x, pl.ds(PY + ny - 1, 1), mid_z]
+        if c == 0:
+            ysend[slot, HIGH, x - 1] = d[slot, x, pl.ds(PY, 1), mid_z]
+
+    def unpack(slot, x, c):
+        if c == 0:
+            d[slot, x, pl.ds(PY - 1, 1), mid_z] = yrecv[slot, LOW, x - 1]
+        if c == CHUNKS - 1:
+            d[slot, x, pl.ds(PY + ny, 1), mid_z] = yrecv[slot, HIGH, x - 1]
 
     def block(k, x, y):
         slot, other = k % 2, (k + 1) % 2
@@ -253,65 +291,65 @@
     def add(total, term):
         return total if term is None else total + term
 
-    for side in (LOW, HIGH):
-        for c in range(CHUNKS):
-            x_copy(0, side, c, rhs).start()
-    load_rhs.wait()
+    load_rhs[0].wait()
+    load_rhs[1].wait()
+    for c in order:
+        for side in (LOW, HIGH):
+            x_copy(0, side, c).start()
+    load_rhs[2].wait()
 
     def pack_first(x, carry):
-        pack(0, x)
+        for c in (0, CHUNKS - 1):
+            pack(0, x, c)
         return carry
 
     lax.fori_loop(1, nx + 1, pack_first, 0)
-    open_each(0, (INNER, LOW, HIGH), "start")
-    for copy in loads:
-        copy.wait()
+    for c in order:
+        open_each(0, c, "start")
 
     total = jnp.zeros((ROWS, nz), jnp.float32)
     for k in range(ITERS):
         slot, other = k % 2, (k + 1) % 2
         more = k + 1 < ITERS
-        open_each(slot, (INNER,), "wait_recv")
-        if k > 0:
-            open_each(other, (INNER,), "wait_send")
-
-        def inner(x, total, k=k, slot=slot, other=other, more=more):
-            unpack(slot, x)
-            for y in range(0, ny, ROWS):
-                total = add(total, block(k, x, y))
-            if more:
-                pack(other, x)
-            return total
-
-        total = lax.fori_loop(2, nx, inner, total)
-        if more:
-            open_each(other, (INNER,), "start")
-        open_each(slot, (LOW, HIGH), "wait_recv")
-        if k > 0:
-            open_each(other, (LOW, HIGH), "wait_send")
-        unpack(slot, 1)
-        unpack(slot, nx)
-        for c in range(CHUNKS):
+        for c in order:
+            if k == 0:
+                for copy in loads[c]:
+                    copy.wait()
+            open_each(slot, c, "wait_recv")
+            if k > 0:
+                open_each(other, c, "wait_send")
+                for side in (LOW, HIGH):
+                    x_copy(other, side, c).wait_send()
+
+            def planes(xs, total, k=k, c=c, slot=slot, other=other, more=more):
+                for x in xs:
+                    unpack(slot, x, c)
+                for x in xs:
+                    for y in range(c * chunk, (c + 1) * chunk, ROWS):
+                        total = add(total, block(k, x, y))
+                if more:
+                    for x in xs:
+                        pack(other, x, c)
+                return total
+
+            def group(i, total, planes=planes):
+                return planes([2 + i * GROUP + j for j in range(GROUP)], total)
+
+            total = lax.fori_loop(0, (nx - 2) // GROUP, group, total)
             for side in (LOW, HIGH):
                 x_copy(slot, side, c).wait_recv()
-                if k > 0:
-                    x_copy(other, side, c, rhs if k == 1 else None).wait_send()
-            for x in (1, nx):
-                for y in range(c * chunk, (c + 1) * chunk, ROWS):
-                    total = add(total, block(k, x, y))
+            total = planes((1, nx), total)
             if more:
                 for side in (LOW, HIGH):
                     x_copy(other, side, c).start()
-        if more:
-            pack(other, 1)
-            pack(other, nx)
-            open_each(other, (LOW, HIGH), "start")
+                open_each(other, c, "start")
 
     tile = total[:, :PZ]
     for z in range(PZ, nz, PZ):
         tile = tile + total[:, z : z + PZ]
+    tile = jnp.sum(tile, axis=0, keepdims=True)
     first = 0
-    for axes in PHASES:
+    for axes in phases(sizes):
         group = phase_steps(sizes, axes)
         own = jnp.int32(0)
         for axis in axes:
@@ -339,13 +377,30 @@
             copy.wait_send()
         first += len(group) + 1
     last = (ITERS - 1) % 2
-    open_each(last, (INNER, LOW, HIGH), "wait_send")
-    for c in range(CHUNKS):
+    for c in order:
+        open_each(last, c, "wait_send")
         for side in (LOW, HIGH):
             x_copy(last, side, c).wait_send()
     cells = nx * ny * nz * sizes[0] * sizes[1] * sizes[2]
     mean = jnp.sum(tile, keepdims=True) / cells
     norm[...] = jnp.sqrt(mean + 1e-06)
+
+
+def put_out(sol, res, sol_out, res_out, sem):
+    part = sol.shape[0] // 4
+    copies = [
+        pltpu.make_async_copy(
+            source.at[pl.ds(i * part, part)],
+            target.at[pl.ds(i * part, part)],
+            sem.at[j, i],
+        )
+        for i in range(4)
+        for j, (source, target) in enumerate(((sol, sol_out), (res, res_out)))
+    ]
+    for copy in copies:
+        copy.start()
+    for copy in copies:
+        copy.wait()
 
 
 def local(sizes, right_side, reaction, velocity):
@@ -365,14 +420,15 @@
             pltpu.VMEM((3, nx, ny, nz), jnp.float32),
             pltpu.VMEM((2, 2, nx, 1, nz), jnp.float32),
             pltpu.VMEM((2, 2, nx, 1, nz), jnp.float32),
-            pltpu.VMEM((phase_slots(sizes), ROWS, PZ), jnp.float32),
-            dma((5,)),
+            pltpu.VMEM((phase_slots(sizes), 1, PZ), jnp.float32),
+            dma((3,)),
+            dma((CHUNKS, 2)),
             dma((2, 2, CHUNKS)),
             dma((2, 2, CHUNKS)),
-            dma((2, 2, 3)),
-            dma((2, 2, 3)),
-            dma((2, 2, 3)),
-            dma((2, 2, 3)),
+            dma((2, 2)),
+            dma((2, 2)),
+            dma((2, 2, CHUNKS)),
+            dma((2, 2, CHUNKS)),
             dma((phase_slots(sizes),)),
             dma((phase_slots(sizes),)),
         ],
@@ -387,6 +443,14 @@
             for a in (right_side, reaction, velocity)
         )
     )
+    sol, res = pl.pallas_call(
+        put_out,
+        out_shape=(field, field),
+        in_specs=[vmem] * 2,
+        out_specs=(hbm, hbm),
+        scratch_shapes=[dma((2, 4))],
+        compiler_params=pltpu.CompilerParams(vmem_limit_bytes=16 * 1024 * 1024),
+    )(sol, res)
     return sol, res, norm[0, 0]
 
 

time: 48.4 us -> 46.9 us (0.969)
  local copies, waits for them, and re-layouts: 2.64 us -> 0 us
  Pallas kernels: 43.3 us -> 44.3 us
    unnamed x2 -> x0, local copies, waits for them, and re-layouts: 2.64 us -> none
    pallas_call x0 -> x1, Pallas kernels: none -> 2.07 us  [local(): pl.pallas_call(put_out, out_shape=(field, field), in_specs=[vmem] * 2, ou...]
    pallas_call x1, Pallas kernels: 43.3 us -> 42.3 us  [local(): pl.pallas_call(functools.partial(kernel, sizes), out_shape=(field, field,...]
where the time goes in v1:
time: 46.9 us; the launch traced here: 46.7 us
  Pallas kernels  44.3 us (94%)
  between operations  2.4 us (5%)
    pallas_call x1, Pallas kernels, local(): pl.pallas_call(functools.partial(kernel, sizes), out_shape=(field, field,...  42.3 us
    pallas_call x1, Pallas kernels, local(): pl.pallas_call(put_out, out_shape=(field, field), in_specs=[vmem] * 2, ou...  2.07 us

profile of v1, /device:TPU:0, one launch (start us, length us, event | category | flops | bytes accessed | tf_op | source)
XLA Modules:
  0.0 46.7 jit_solution(4187801968887167576)
XLA Ops:
  0.6 42.3 %shard_map.58 = (f32[16,64,512]{2,1,0:T(8,128)S(1)}, f32[16,64,512]{2,1,0:T(8,128)S(1)}, f32[1,1]{1,0:T(1,128)}) custom-call(f32[16,64,512]{2,1,0:T(8,128)} %rhs.1, f32[16,64,512]{2,1,0:T(8,128)} %reaction.1, f32[3,16,64,512]{3,2,1,0:T(8,128)} %velocity.1), custom_call_target="tpu_custom_call" | custom-call | tf_op jit(solution)/shard_map/pallas_call | solution.py:412
  42.9 2.1 %shard_map.59 = (f32[16,64,512]{2,1,0:T(8,128)}, f32[16,64,512]{2,1,0:T(8,128)}) custom-call(f32[16,64,512]{2,1,0:T(8,128)S(1)} %get-tuple-element.8.sol, f32[16,64,512]{2,1,0:T(8,128)S(1)} %get-tuple-element.9.res), custom_call_target="tpu_custom_call" | custom-call | tf_op jit(solution)/shard_map/pallas_call | solution.py:446

commit v2 on v1

--- a/solution.py
+++ b/solution.py
@@ -66,8 +66,7 @@
     res,
     norm,
     d,
-    reac,
-    vel,
+    coef,
     ysend,
     yrecv,
     part,
@@ -89,32 +88,6 @@
     mid_z = pl.ds(PZ, nz)
     chunk = ny // CHUNKS
 
-    order = [0, CHUNKS - 1] + list(range(1, CHUNKS - 1))
-    load_rhs = [
-        pltpu.make_async_copy(
-            rhs.at[pl.ds(first, count)],
-            d.at[0, pl.ds(1 + first, count), mid_y, mid_z],
-            rhs_sem.at[i],
-        )
-        for i, (first, count) in enumerate(((0, 1), (nx - 1, 1), (1, nx - 2)))
-    ]
-    loads = {}
-    for c in order:
-        rows = pl.ds(c * chunk, chunk)
-        loads[c] = [
-            pltpu.make_async_copy(
-                reaction.at[:, rows], reac.at[:, rows], load_sem.at[c, 0]
-            ),
-            pltpu.make_async_copy(
-                velocity.at[:, :, rows], vel.at[:, :, rows], load_sem.at[c, 1]
-            ),
-        ]
-    for copy in load_rhs:
-        copy.start()
-    for c in order:
-        for copy in loads[c]:
-            copy.start()
-
     barrier = pltpu.get_barrier_semaphore()
     def shifted(steps):
         return {
@@ -150,6 +123,34 @@
             greet(steps)
         greeters = len(greeted_by(sizes))
 
+    order = [0, CHUNKS - 1] + list(range(1, CHUNKS - 1))
+    load_rhs = [
+        pltpu.make_async_copy(
+            rhs.at[pl.ds(first, count)],
+            d.at[0, pl.ds(1 + first, count), mid_y, mid_z],
+            rhs_sem.at[i],
+        )
+        for i, (first, count) in enumerate(((0, 1), (nx - 1, 1), (1, nx - 2)))
+    ]
+    loads = {}
+    for c in order:
+        rows = pl.ds(c * chunk, chunk)
+        loads[c] = [
+            pltpu.make_async_copy(
+                reaction.at[:, rows], coef.at[3, :, rows], load_sem.at[c]
+            ),
+            pltpu.make_async_copy(
+                velocity.at[:, :, rows],
+                coef.at[pl.ds(0, 3), :, rows],
+                load_sem.at[c],
+            ),
+        ]
+    for copy in load_rhs:
+        copy.start()
+    for c in order:
+        for copy in loads[c]:
+            copy.start()
+
     for side, at_edge in ((LOW, me[1] == 0), (HIGH, me[1] == sizes[1] - 1)):
         @pl.when(at_edge)
         def _(side=side):
@@ -191,11 +192,18 @@
         return remote(
             d.at[slot, plane, rows, mid_z],
             d.at[slot, land, rows, mid_z],
-            xs_sem.at[slot, side, c],
+            xs_sem.at[slot],
             xr_sem.at[slot, side, c],
             0,
             target,
         )
+
+    def start_x(slot, c):
+        for even, sides in ((True, (HIGH, LOW)), (False, (LOW, HIGH))):
+            @pl.when((lax.rem(me[0], 2) == 0) == even)
+            def _(sides=sides):
+                for side in sides:
+                    x_copy(slot, side, c).start()
 
     def target_of(axis, side):
         n = sizes[axis]
@@ -225,11 +233,26 @@
         return remote(
             d.at[slot, x, rows, pl.ds(source, PZ)],
             d.at[slot, x, rows, pl.ds(land, PZ)],
-            zs_sem.at[slot, side, c],
+            zs_sem.at[slot, side],
             zr_sem.at[slot, side, c],
             2,
             target_of(2, side),
         )
+
+    def sent(slot):
+        both = d.at[slot, pl.ds(0, 2), mid_y, mid_z]
+        remote(both, both, xs_sem.at[slot], xr_sem.at[slot, 0, 0], 0, me[0]).wait_send()
+        for side in (LOW, HIGH):
+            @pl.when(sends(2, side))
+            def _(side=side):
+                edge = d.at[slot, pl.ds(1, nx), mid_y, pl.ds(0, PZ)]
+                remote(
+                    edge, edge, zs_sem.at[slot, side], zr_sem.at[slot, side, 0], 2, me[2]
+                ).wait_send()
+
+            @pl.when(sends(1, side))
+            def _(side=side):
+                y_copy(slot, side).wait_send()
 
     def open_each(slot, c, act):
         rule = receives if act == "wait_recv" else sends
@@ -270,9 +293,9 @@
         pz = pltpu.roll(d[slot, x, rows, pl.ds(PZ, wide)], wide - 1, 1)[:, :nz]
         mz = pltpu.roll(d[slot, x, rows, pl.ds(0, wide)], 1, 1)[:, PZ:]
         beside = ((px + mx) + (py + my)) + (pz + mz)
-        skew = vel[0, *here] * (px - mx) + vel[1, *here] * (py - my)
-        skew = skew + vel[2, *here] * (pz - mz)
-        applied = (6.0 + reac[here]) * mid - (beside - skew)
+        skew = coef[0, *here] * (px - mx) + coef[1, *here] * (py - my)
+        skew = skew + coef[2, *here] * (pz - mz)
+        applied = (6.0 + coef[3, *here]) * mid - (beside - skew)
         if k == 0:
             left = mid - (1.0 / centre) * applied
             sol[here] = (1.0 / centre) * mid
@@ -294,8 +317,7 @@
     load_rhs[0].wait()
     load_rhs[1].wait()
     for c in order:
-        for side in (LOW, HIGH):
-            x_copy(0, side, c).start()
+        start_x(0, c)
     load_rhs[2].wait()
 
     def pack_first(x, carry):
@@ -313,13 +335,11 @@
         more = k + 1 < ITERS
         for c in order:
             if k == 0:
-                for copy in loads[c]:
-                    copy.wait()
+                block_of = coef.at[:, :, pl.ds(c * chunk, chunk)]
+                pltpu.make_async_copy(block_of, block_of, load_sem.at[c]).wait()
             open_each(slot, c, "wait_recv")
-            if k > 0:
-                open_each(other, c, "wait_send")
-                for side in (LOW, HIGH):
-                    x_copy(other, side, c).wait_send()
+            if k > 0 and c == order[0]:
+                sent(other)
 
             def planes(xs, total, k=k, c=c, slot=slot, other=other, more=more):
                 for x in xs:
@@ -340,8 +360,7 @@
                 x_copy(slot, side, c).wait_recv()
             total = planes((1, nx), total)
             if more:
-                for side in (LOW, HIGH):
-                    x_copy(other, side, c).start()
+                start_x(other, c)
                 open_each(other, c, "start")
 
     tile = total[:, :PZ]
@@ -349,53 +368,45 @@
         tile = tile + total[:, z : z + PZ]
     tile = jnp.sum(tile, axis=0, keepdims=True)
     first = 0
-    for axes in phases(sizes):
+    for phase, axes in enumerate(phases(sizes)):
         group = phase_steps(sizes, axes)
         own = jnp.int32(0)
         for axis in axes:
             own = own * sizes[axis] + me[axis]
         part[first + own] = tile
-        copies = [
-            pltpu.make_async_remote_copy(
-                src_ref=part.at[first + own],
-                dst_ref=part.at[first + own],
-                send_sem=ps_sem.at[first + p],
-                recv_sem=pr_sem.at[first + p],
+
+        def message(source, steps):
+            return pltpu.make_async_remote_copy(
+                src_ref=source,
+                dst_ref=source,
+                send_sem=ps_sem.at[phase],
+                recv_sem=pr_sem.at[phase],
                 device_id=shifted(steps),
                 device_id_type=pl.DeviceIdType.MESH,
             )
-            for p, steps in enumerate(group)
-        ]
-        for copy in copies:
-            copy.start()
-        for copy in copies:
-            copy.wait_recv()
+
+        for steps in group:
+            message(part.at[first + own], steps).start()
+        whole = message(part.at[pl.ds(first, len(group))], group[0])
+        if phase == 0:
+            sent((ITERS - 1) % 2)
+        whole.wait_send()
+        whole.wait_recv()
         tile = part[first]
         for p in range(1, len(group) + 1):
             tile = tile + part[first + p]
-        for copy in copies:
-            copy.wait_send()
         first += len(group) + 1
-    last = (ITERS - 1) % 2
-    for c in order:
-        open_each(last, c, "wait_send")
-        for side in (LOW, HIGH):
-            x_copy(last, side, c).wait_send()
     cells = nx * ny * nz * sizes[0] * sizes[1] * sizes[2]
     mean = jnp.sum(tile, keepdims=True) / cells
-    norm[...] = jnp.sqrt(mean + 1e-06)
-
-
-def put_out(sol, res, sol_out, res_out, sem):
-    part = sol.shape[0] // 4
+    norm[...] = jnp.broadcast_to(jnp.sqrt(mean + 1e-06), norm.shape)
+
+
+def put_out(sol, res, norm, sol_out, res_out, norm_out, sem):
     copies = [
-        pltpu.make_async_copy(
-            source.at[pl.ds(i * part, part)],
-            target.at[pl.ds(i * part, part)],
-            sem.at[j, i],
-        )
-        for i in range(4)
-        for j, (source, target) in enumerate(((sol, sol_out), (res, res_out)))
+        pltpu.make_async_copy(source, target, sem.at[i])
+        for i, (source, target) in enumerate(
+            ((sol, sol_out), (res, res_out), (norm, norm_out))
+        )
     ]
     for copy in copies:
         copy.start()
@@ -411,26 +422,25 @@
     field = jax.ShapeDtypeStruct((nx, ny, nz), jnp.float32)
     sol, res, norm = pl.pallas_call(
         functools.partial(kernel, sizes),
-        out_shape=(field, field, jax.ShapeDtypeStruct((1, 1), jnp.float32)),
+        out_shape=(field, field, jax.ShapeDtypeStruct((1, PZ), jnp.float32)),
         in_specs=[hbm] * 3,
         out_specs=(vmem, vmem, vmem),
         scratch_shapes=[
             pltpu.VMEM((2, nx + 2, ny + 2 * PY, nz + 2 * PZ), jnp.float32),
-            pltpu.VMEM((nx, ny, nz), jnp.float32),
-            pltpu.VMEM((3, nx, ny, nz), jnp.float32),
+            pltpu.VMEM((4, nx, ny, nz), jnp.float32),
             pltpu.VMEM((2, 2, nx, 1, nz), jnp.float32),
             pltpu.VMEM((2, 2, nx, 1, nz), jnp.float32),
             pltpu.VMEM((phase_slots(sizes), 1, PZ), jnp.float32),
             dma((3,)),
-            dma((CHUNKS, 2)),
-            dma((2, 2, CHUNKS)),
+            dma((CHUNKS,)),
+            dma((2,)),
             dma((2, 2, CHUNKS)),
             dma((2, 2)),
             dma((2, 2)),
+            dma((2, 2)),
             dma((2, 2, CHUNKS)),
-            dma((2, 2, CHUNKS)),
-            dma((phase_slots(sizes),)),
-            dma((phase_slots(sizes),)),
+            dma((len(phases(sizes)),)),
+            dma((len(phases(sizes)),)),
         ],
         compiler_params=pltpu.CompilerParams(
             collective_id=0,
@@ -443,14 +453,14 @@
             for a in (right_side, reaction, velocity)
         )
     )
-    sol, res = pl.pallas_call(
+    sol, res, norm = pl.pallas_call(
         put_out,
-        out_shape=(field, field),
-        in_specs=[vmem] * 2,
-        out_specs=(hbm, hbm),
-        scratch_shapes=[dma((2, 4))],
+        out_shape=(field, field, jax.ShapeDtypeStruct((1, PZ), jnp.float32)),
+        in_specs=[vmem] * 3,
+        out_specs=(hbm,) * 3,
+        scratch_shapes=[dma((3,))],
         compiler_params=pltpu.CompilerParams(vmem_limit_bytes=16 * 1024 * 1024),
-    )(sol, res)
+    )(sol, res, norm)
     return sol, res, norm[0, 0]
 
 

time: 46.9 us -> 43.3 us (0.923)
  Pallas kernels: 44.3 us -> 42.5 us
  between operations: 2.4 us -> 0.64 us
    pallas_call x1, Pallas kernels: 42.3 us -> 40.4 us  [local(): pl.pallas_call(functools.partial(kernel, sizes), out_shape=(field, field,...]
where the time goes in v2:
time: 43.3 us; the launch traced here: 43.1 us
  Pallas kernels  42.5 us (98%)
  between operations  0.64 us (1%)
    pallas_call x1, Pallas kernels, local(): pl.pallas_call(functools.partial(kernel, sizes), out_shape=(field, field,...  40.4 us
    pallas_call x1, Pallas kernels, local(): pl.pallas_call(put_out, out_shape=(field, field, jax.ShapeDtypeStruct((1,...  2.04 us

profile of v2, /device:TPU:0, one launch (start us, length us, event | category | flops | bytes accessed | tf_op | source)
XLA Modules:
  0.0 43.1 jit_solution(2514373781807654387)
XLA Ops:
  0.6 40.4 %shard_map.58 = (f32[16,64,512]{2,1,0:T(8,128)S(1)}, f32[16,64,512]{2,1,0:T(8,128)S(1)}, f32[1,128]{1,0:T(1,128)S(1)}) custom-call(f32[16,64,512]{2,1,0:T(8,128)} %rhs.1, f32[16,64,512]{2,1,0:T(8,128)} %reaction.1, f32[3,16,64,512]{3,2,1,0:T(8,128)} %velocity.1), custom_call_target="tpu_custom_call" | custom-call | tf_op jit(solution)/shard_map/pallas_call | solution.py:423
  41.1 2.0 %shard_map.59 = (f32[16,64,512]{2,1,0:T(8,128)}, f32[16,64,512]{2,1,0:T(8,128)}, f32[1,128]{1,0:T(1,128)}) custom-call(f32[16,64,512]{2,1,0:T(8,128)S(1)} %get-tuple-element.9.sol, f32[16,64,512]{2,1,0:T(8,128)S(1)} %get-tuple-element.10.res, f32[1,128]{1,0:T(1,128)S(1)} %get-tuple-element.11.norm), custom_call_target="tpu_custom_call" | custom-call | tf_op jit(solution)/shard_map/pallas_call | solution.py:456

commit v3 on v2

--- a/solution.py
+++ b/solution.py
@@ -9,9 +9,11 @@
 from jax.sharding import PartitionSpec as P
 
 ITERS = 5
-CHUNKS = 4
+CHUNKS = 3
+FIRST, LAST = 0, 1
 ROWS = 8
 GROUP = 7
+EDGE = 2
 
 centre = 7.25
 half_width = 6.75
@@ -19,6 +21,11 @@
 AXES = ("gx", "gy", "gz")
 PY, PZ = 8, 128
 LOW, HIGH = 0, 1
+
+
+def row_chunks(ny):
+    edge = EDGE * (ny // ROWS) // 8 * ROWS
+    return [(0, edge), (ny - edge, edge), (edge, ny - 2 * edge)]
 
 
 def chebyshev_weights(count):
@@ -39,7 +46,9 @@
 
 def phase_steps(sizes, axes):
     ranges = [range(n) if i in axes else (0,) for i, n in enumerate(sizes)]
-    return [steps for steps in itertools.product(*ranges) if any(steps)]
+    found = [steps for steps in itertools.product(*ranges) if any(steps)]
+    hops = lambda steps: min(steps[0], sizes[0] - steps[0]) + sum(steps[1:])
+    return sorted(found, key=hops, reverse=True)
 
 
 def greeted_by(sizes):
@@ -64,7 +73,7 @@
     velocity,
     sol,
     res,
-    norm,
+    sums,
     d,
     coef,
     ysend,
@@ -86,7 +95,7 @@
     me = [lax.axis_index(a) for a in AXES]
     mid_y = pl.ds(PY, ny)
     mid_z = pl.ds(PZ, nz)
-    chunk = ny // CHUNKS
+    chunks = row_chunks(ny)
 
     barrier = pltpu.get_barrier_semaphore()
     def shifted(steps):
@@ -123,18 +132,18 @@
             greet(steps)
         greeters = len(greeted_by(sizes))
 
-    order = [0, CHUNKS - 1] + list(range(1, CHUNKS - 1))
+    order = range(CHUNKS)
     load_rhs = [
         pltpu.make_async_copy(
             rhs.at[pl.ds(first, count)],
             d.at[0, pl.ds(1 + first, count), mid_y, mid_z],
-            rhs_sem.at[i],
+            rhs_sem.at[i // 2],
         )
         for i, (first, count) in enumerate(((0, 1), (nx - 1, 1), (1, nx - 2)))
     ]
     loads = {}
     for c in order:
-        rows = pl.ds(c * chunk, chunk)
+        rows = pl.ds(*chunks[c])
         loads[c] = [
             pltpu.make_async_copy(
                 reaction.at[:, rows], coef.at[3, :, rows], load_sem.at[c]
@@ -183,7 +192,7 @@
 
     def x_copy(slot, side, c):
         n = sizes[0]
-        rows = pl.ds(PY + c * chunk, chunk)
+        rows = pl.ds(PY + chunks[c][0], chunks[c][1])
         plane, land, target = (
             (nx, 0, lax.rem(me[0] + 1, n))
             if side == LOW
@@ -228,7 +237,7 @@
 
     def z_copy(slot, side, c):
         x = pl.ds(1, nx)
-        rows = pl.ds(PY + c * chunk, chunk)
+        rows = pl.ds(PY + chunks[c][0], chunks[c][1])
         source, land = (nz, 0) if side == LOW else (PZ, PZ + nz)
         return remote(
             d.at[slot, x, rows, pl.ds(source, PZ)],
@@ -257,7 +266,7 @@
     def open_each(slot, c, act):
         rule = receives if act == "wait_recv" else sends
         for side in (LOW, HIGH):
-            row_in = CHUNKS - 1 if side == LOW and act != "wait_recv" else 0
+            row_in = LAST if side == LOW and act != "wait_recv" else FIRST
 
             @pl.when(rule(2, side))
             def _(side=side):
@@ -269,15 +278,15 @@
                     getattr(y_copy(slot, side), act)()
 
     def pack(slot, x, c):
-        if c == CHUNKS - 1:
+        if c == LAST:
             ysend[slot, LOW, x - 1] = d[slot, x, pl.ds(PY + ny - 1, 1), mid_z]
-        if c == 0:
+        if c == FIRST:
             ysend[slot, HIGH, x - 1] = d[slot, x, pl.ds(PY, 1), mid_z]
 
     def unpack(slot, x, c):
-        if c == 0:
+        if c == FIRST:
             d[slot, x, pl.ds(PY - 1, 1), mid_z] = yrecv[slot, LOW, x - 1]
-        if c == CHUNKS - 1:
+        if c == LAST:
             d[slot, x, pl.ds(PY + ny, 1), mid_z] = yrecv[slot, HIGH, x - 1]
 
     def block(k, x, y):
@@ -314,14 +323,14 @@
     def add(total, term):
         return total if term is None else total + term
 
-    load_rhs[0].wait()
-    load_rhs[1].wait()
+    two = d.at[0, pl.ds(1, 2), mid_y, mid_z]
+    pltpu.make_async_copy(two, two, rhs_sem.at[0]).wait()
     for c in order:
         start_x(0, c)
     load_rhs[2].wait()
 
     def pack_first(x, carry):
-        for c in (0, CHUNKS - 1):
+        for c in (FIRST, LAST):
             pack(0, x, c)
         return carry
 
@@ -335,7 +344,7 @@
         more = k + 1 < ITERS
         for c in order:
             if k == 0:
-                block_of = coef.at[:, :, pl.ds(c * chunk, chunk)]
+                block_of = coef.at[:, :, pl.ds(*chunks[c])]
                 pltpu.make_async_copy(block_of, block_of, load_sem.at[c]).wait()
             open_each(slot, c, "wait_recv")
             if k > 0 and c == order[0]:
@@ -345,7 +354,7 @@
                 for x in xs:
                     unpack(slot, x, c)
                 for x in xs:
-                    for y in range(c * chunk, (c + 1) * chunk, ROWS):
+                    for y in range(chunks[c][0], sum(chunks[c]), ROWS):
                         total = add(total, block(k, x, y))
                 if more:
                     for x in xs:
@@ -396,20 +405,21 @@
         for p in range(1, len(group) + 1):
             tile = tile + part[first + p]
         first += len(group) + 1
-    cells = nx * ny * nz * sizes[0] * sizes[1] * sizes[2]
-    mean = jnp.sum(tile, keepdims=True) / cells
-    norm[...] = jnp.broadcast_to(jnp.sqrt(mean + 1e-06), norm.shape)
-
-
-def put_out(sol, res, norm, sol_out, res_out, norm_out, sem):
+    sums[...] = tile
+
+
+def put_out(cells, sol, res, sums, sol_out, res_out, norm_out, norm, sem):
     copies = [
         pltpu.make_async_copy(source, target, sem.at[i])
         for i, (source, target) in enumerate(
             ((sol, sol_out), (res, res_out), (norm, norm_out))
         )
     ]
-    for copy in copies:
-        copy.start()
+    copies[0].start()
+    copies[1].start()
+    mean = jnp.sum(sums[...], keepdims=True) / cells
+    norm[...] = jnp.broadcast_to(jnp.sqrt(mean + 1e-06), norm.shape)
+    copies[2].start()
     for copy in copies:
         copy.wait()
 
@@ -420,7 +430,7 @@
     vmem = pl.BlockSpec(memory_space=pltpu.VMEM)
     dma = pltpu.SemaphoreType.DMA
     field = jax.ShapeDtypeStruct((nx, ny, nz), jnp.float32)
-    sol, res, norm = pl.pallas_call(
+    sol, res, sums = pl.pallas_call(
         functools.partial(kernel, sizes),
         out_shape=(field, field, jax.ShapeDtypeStruct((1, PZ), jnp.float32)),
         in_specs=[hbm] * 3,
@@ -431,7 +441,7 @@
             pltpu.VMEM((2, 2, nx, 1, nz), jnp.float32),
             pltpu.VMEM((2, 2, nx, 1, nz), jnp.float32),
             pltpu.VMEM((phase_slots(sizes), 1, PZ), jnp.float32),
-            dma((3,)),
+            dma((2,)),
             dma((CHUNKS,)),
             dma((2,)),
             dma((2, 2, CHUNKS)),
@@ -453,14 +463,15 @@
             for a in (right_side, reaction, velocity)
         )
     )
+    cells = nx * ny * nz * sizes[0] * sizes[1] * sizes[2]
     sol, res, norm = pl.pallas_call(
-        put_out,
+        functools.partial(put_out, cells),
         out_shape=(field, field, jax.ShapeDtypeStruct((1, PZ), jnp.float32)),
         in_specs=[vmem] * 3,
         out_specs=(hbm,) * 3,
-        scratch_shapes=[dma((3,))],
+        scratch_shapes=[pltpu.VMEM((1, PZ), jnp.float32), dma((3,))],
         compiler_params=pltpu.CompilerParams(vmem_limit_bytes=16 * 1024 * 1024),
-    )(sol, res, norm)
+    )(sol, res, sums)
     return sol, res, norm[0, 0]
 
 

time: 43.3 us -> 42.8 us (0.988)
  Pallas kernels: 42.5 us -> 42 us
where the time goes in v3:
time: 42.8 us; the launch traced here: 42.7 us
  Pallas kernels  42 us (98%)
  between operations  0.64 us (1%)
    pallas_call x1, Pallas kernels, local(): pl.pallas_call(functools.partial(kernel, sizes), out_shape=(field, field,...  40 us
    pallas_call x1, Pallas kernels, local(): pl.pallas_call(functools.partial(put_out, cells), out_shape=(field, field...  2.04 us

profile of v3, /device:TPU:0, one launch (start us, length us, event | category | flops | bytes accessed | tf_op | source)
XLA Modules:
  0.0 42.7 jit_solution(11153862326019678653)
XLA Ops:
  0.6 40.0 %shard_map.58 = (f32[16,64,512]{2,1,0:T(8,128)S(1)}, f32[16,64,512]{2,1,0:T(8,128)S(1)}, f32[1,128]{1,0:T(1,128)S(1)}) custom-call(f32[16,64,512]{2,1,0:T(8,128)} %rhs.1, f32[16,64,512]{2,1,0:T(8,128)} %reaction.1, f32[3,16,64,512]{3,2,1,0:T(8,128)} %velocity.1), custom_call_target="tpu_custom_call" | custom-call | tf_op jit(solution)/shard_map/pallas_call | solution.py:433
  40.6 2.0 %shard_map.59 = (f32[16,64,512]{2,1,0:T(8,128)}, f32[16,64,512]{2,1,0:T(8,128)}, f32[1,128]{1,0:T(1,128)}) custom-call(f32[16,64,512]{2,1,0:T(8,128)S(1)} %get-tuple-element.9.sol, f32[16,64,512]{2,1,0:T(8,128)S(1)} %get-tuple-element.10.res, f32[1,128]{1,0:T(1,128)S(1)} %get-tuple-element.11.sums), custom_call_target="tpu_custom_call" | custom-call | tf_op jit(solution)/shard_map/pallas_call | solution.py:467

commit v4 on v3

--- a/solution.py
+++ b/solution.py
@@ -133,6 +133,11 @@
         greeters = len(greeted_by(sizes))
 
     order = range(CHUNKS)
+
+    def landed(c, base=0):
+        start, count = chunks[c]
+        return pl.ds(base + start, 2 * count if c == FIRST else count)
+
     load_rhs = [
         pltpu.make_async_copy(
             rhs.at[pl.ds(first, count)],
@@ -146,12 +151,12 @@
         rows = pl.ds(*chunks[c])
         loads[c] = [
             pltpu.make_async_copy(
-                reaction.at[:, rows], coef.at[3, :, rows], load_sem.at[c]
+                reaction.at[:, rows], coef.at[3, :, rows], load_sem.at[c // 2]
             ),
             pltpu.make_async_copy(
                 velocity.at[:, :, rows],
                 coef.at[pl.ds(0, 3), :, rows],
-                load_sem.at[c],
+                load_sem.at[c // 2],
             ),
         ]
     for copy in load_rhs:
@@ -235,15 +240,15 @@
             target_of(1, side),
         )
 
-    def z_copy(slot, side, c):
+    def z_copy(slot, side, c, rows=None):
         x = pl.ds(1, nx)
-        rows = pl.ds(PY + chunks[c][0], chunks[c][1])
+        rows = pl.ds(PY + chunks[c][0], chunks[c][1]) if rows is None else rows
         source, land = (nz, 0) if side == LOW else (PZ, PZ + nz)
         return remote(
             d.at[slot, x, rows, pl.ds(source, PZ)],
             d.at[slot, x, rows, pl.ds(land, PZ)],
             zs_sem.at[slot, side],
-            zr_sem.at[slot, side, c],
+            zr_sem.at[slot, side, c // 2],
             2,
             target_of(2, side),
         )
@@ -268,9 +273,11 @@
         for side in (LOW, HIGH):
             row_in = LAST if side == LOW and act != "wait_recv" else FIRST
 
-            @pl.when(rule(2, side))
-            def _(side=side):
-                getattr(z_copy(slot, side, c), act)()
+            if act == "start" or c != LAST:
+                @pl.when(rule(2, side))
+                def _(side=side):
+                    rows = None if act == "start" else landed(c, PY)
+                    getattr(z_copy(slot, side, c, rows), act)()
 
             if c == row_in:
                 @pl.when(rule(1, side))
@@ -344,8 +351,11 @@
         more = k + 1 < ITERS
         for c in order:
             if k == 0:
-                block_of = coef.at[:, :, pl.ds(*chunks[c])]
-                pltpu.make_async_copy(block_of, block_of, load_sem.at[c]).wait()
+                if c != LAST:
+                    block_of = coef.at[:, :, landed(c)]
+                    pltpu.make_async_copy(
+                        block_of, block_of, load_sem.at[c // 2]
+                    ).wait()
             open_each(slot, c, "wait_recv")
             if k > 0 and c == order[0]:
                 sent(other)
@@ -442,13 +452,13 @@
             pltpu.VMEM((2, 2, nx, 1, nz), jnp.float32),
             pltpu.VMEM((phase_slots(sizes), 1, PZ), jnp.float32),
             dma((2,)),
-            dma((CHUNKS,)),
+            dma((2,)),
             dma((2,)),
             dma((2, 2, CHUNKS)),
             dma((2, 2)),
             dma((2, 2)),
             dma((2, 2)),
-            dma((2, 2, CHUNKS)),
+            dma((2, 2, 2)),
             dma((len(phases(sizes)),)),
             dma((len(phases(sizes)),)),
         ],

time: 42.8 us -> 42.8 us (level)
  no operation moved by 1% of the time
where the time goes in v4:
time: 42.8 us; the launch traced here: 42.6 us
  Pallas kernels  42 us (98%)
  between operations  0.64 us (1%)
    pallas_call x1, Pallas kernels, local(): pl.pallas_call(functools.partial(kernel, sizes), out_shape=(field, field,...  40 us
    pallas_call x1, Pallas kernels, local(): pl.pallas_call(functools.partial(put_out, cells), out_shape=(field, field...  2.04 us

profile of v4, /device:TPU:0, one launch (start us, length us, event | category | flops | bytes accessed | tf_op | source)
XLA Modules:
  0.0 42.6 jit_solution(1683987592889542855)
XLA Ops:
  0.6 40.0 %shard_map.58 = (f32[16,64,512]{2,1,0:T(8,128)S(1)}, f32[16,64,512]{2,1,0:T(8,128)S(1)}, f32[1,128]{1,0:T(1,128)S(1)}) custom-call(f32[16,64,512]{2,1,0:T(8,128)} %rhs.1, f32[16,64,512]{2,1,0:T(8,128)} %reaction.1, f32[3,16,64,512]{3,2,1,0:T(8,128)} %velocity.1), custom_call_target="tpu_custom_call" | custom-call | tf_op jit(solution)/shard_map/pallas_call | solution.py:443
  40.6 2.0 %shard_map.59 = (f32[16,64,512]{2,1,0:T(8,128)}, f32[16,64,512]{2,1,0:T(8,128)}, f32[1,128]{1,0:T(1,128)}) custom-call(f32[16,64,512]{2,1,0:T(8,128)S(1)} %get-tuple-element.9.sol, f32[16,64,512]{2,1,0:T(8,128)S(1)} %get-tuple-element.10.res, f32[1,128]{1,0:T(1,128)S(1)} %get-tuple-element.11.sums), custom_call_target="tpu_custom_call" | custom-call | tf_op jit(solution)/shard_map/pallas_call | solution.py:477

commit v5 on v4

--- a/solution.py
+++ b/solution.py
@@ -247,8 +247,8 @@
         return remote(
             d.at[slot, x, rows, pl.ds(source, PZ)],
             d.at[slot, x, rows, pl.ds(land, PZ)],
-            zs_sem.at[slot, side],
-            zr_sem.at[slot, side, c // 2],
+            zs_sem.at[slot],
+            zr_sem.at[slot, c // 2],
             2,
             target_of(2, side),
         )
@@ -261,7 +261,7 @@
             def _(side=side):
                 edge = d.at[slot, pl.ds(1, nx), mid_y, pl.ds(0, PZ)]
                 remote(
-                    edge, edge, zs_sem.at[slot, side], zr_sem.at[slot, side, 0], 2, me[2]
+                    edge, edge, zs_sem.at[slot], zr_sem.at[slot, 0], 2, me[2]
                 ).wait_send()
 
             @pl.when(sends(1, side))
@@ -457,8 +457,8 @@
             dma((2, 2, CHUNKS)),
             dma((2, 2)),
             dma((2, 2)),
+            dma((2,)),
             dma((2, 2)),
-            dma((2, 2, 2)),
             dma((len(phases(sizes)),)),
             dma((len(phases(sizes)),)),
         ],

time: 42.8 us -> 42.7 us (level)
  no operation moved by 1% of the time
where the time goes in v5:
time: 42.7 us; the launch traced here: 42.6 us
  Pallas kernels  42 us (98%)
  between operations  0.64 us (1%)
    pallas_call x1, Pallas kernels, local(): pl.pallas_call(functools.partial(kernel, sizes), out_shape=(field, field,...  39.9 us
    pallas_call x1, Pallas kernels, local(): pl.pallas_call(functools.partial(put_out, cells), out_shape=(field, field...  2.04 us

profile of v5, /device:TPU:0, one launch (start us, length us, event | category | flops | bytes accessed | tf_op | source)
XLA Modules:
  0.0 42.6 jit_solution(296865331930223508)
XLA Ops:
  0.6 39.9 %shard_map.58 = (f32[16,64,512]{2,1,0:T(8,128)S(1)}, f32[16,64,512]{2,1,0:T(8,128)S(1)}, f32[1,128]{1,0:T(1,128)S(1)}) custom-call(f32[16,64,512]{2,1,0:T(8,128)} %rhs.1, f32[16,64,512]{2,1,0:T(8,128)} %reaction.1, f32[3,16,64,512]{3,2,1,0:T(8,128)} %velocity.1), custom_call_target="tpu_custom_call" | custom-call | tf_op jit(solution)/shard_map/pallas_call | solution.py:443
  40.5 2.0 %shard_map.59 = (f32[16,64,512]{2,1,0:T(8,128)}, f32[16,64,512]{2,1,0:T(8,128)}, f32[1,128]{1,0:T(1,128)}) custom-call(f32[16,64,512]{2,1,0:T(8,128)S(1)} %get-tuple-element.9.sol, f32[16,64,512]{2,1,0:T(8,128)S(1)} %get-tuple-element.10.res, f32[1,128]{1,0:T(1,128)S(1)} %get-tuple-element.11.sums), custom_call_target="tpu_custom_call" | custom-call | tf_op jit(solution)/shard_map/pallas_call | solution.py:477
